TPU v7x, 32 devices: a whole 2x2x4 slice. The times are simulated.
32 devices in a mesh: edge: 8 (over z, y), chan: 4 (over x, core).
Axes of the slice: x: 2, y: 2, z: 4, core: 2. Of those that a mesh axis runs over, the one named last changes fastest.
Arguments:
- node_states: bfloat16 [128, 49, 256], P('edge', None, 'chan'), may hold values from -6 to 6
- edge_vectors: float32 [3, 4096], P(None, ('edge', 'chan')), may hold values from -5.6 to 5.6, as said below
- source_part: int32 [4096, 1], P('edge'), may hold values from 0 to 7; in each aligned block of 512 rows (0 to 511, 512 to 1023, ...) at most 128 rows name the same one
- source_slot: int32 [4096], P('edge'), may hold values from 0 to 15
- target_slot: int32 [4096], P('edge'), may hold values from 0 to 15
- live_edges: int32 [8], P('edge'), may hold values from 1 to 512, 3072 in all
- weight_zero: bfloat16 [7, 256, 7, 256], P(None, 'chan'), may hold values from -0.125 to 0.125
- weight_one: bfloat16 [2, 6, 256, 6, 256], P(None, None, 'chan'), may hold values from -0.109375 to 0.109375
- weight_two: bfloat16 [2, 5, 256, 5, 256], P(None, None, 'chan'), may hold values from -0.125 to 0.125
Outputs:
- aggregated: bfloat16 [128, 49, 256], P('edge', None, 'chan')
Inputs may be any that keep to these rules, and one draw needn't show every extreme that they name: `source_part`: in each aligned block of 512 rows (the edges of one partition's slab) no partition number appears more than 128 times, and some number appears exactly 128 times. Edges are grouped by destination partition: the destination of an edge in slab p is node p * 16 + target_slot. `live_edges`: live slots stand at the front of each slab; the fullest slab is full. `edge_vectors`: every column has length between 0.8 and 5.6.
All inputs are finite; a program needn't handle non-finite values. No bound on the sum of `live_edges` on one device may be relied on, other than what follows from the above.
Results may differ from a plain program's by a relative error of at most 0.015.
Values may be sent and summed in bfloat16 or wider, within the bound.
A program may use at most 128 MiB of HBM per device.

v0:
```python
import math

import jax
import jax.numpy as jnp
import numpy as np
from jax import lax
from jax.experimental import pallas as pl
from jax.experimental.pallas import tpu as pltpu
from jax.sharding import PartitionSpec as P

LMAX = 6
MMAX = 2
COEFS = (LMAX + 1) ** 2
ORDERS = (0, 1, -1, 2, -2)
CUTOFF = 6.0
MESH = pl.DeviceIdType.MESH
LANES = 128


def normalizer(degree, order):
    return math.sqrt(
        (2 * degree + 1)
        / (4.0 * math.pi)
        * math.factorial(degree - order)
        / math.factorial(degree + order)
    )


def harmonics(x, y, z):
    results = {}
    power = [x * 0 + 1 + 0j]
    for _ in range(LMAX):
        power.append(power[-1] * (x + 1j * y))
    for order in range(LMAX + 1):
        start = (-1.0) ** order * math.prod(range(2 * order - 1, 0, -2))
        legendre = {order: z * 0 + start}
        if order < LMAX:
            legendre[order + 1] = (2 * order + 1) * z * start
        for degree in range(order + 2, LMAX + 1):
            legendre[degree] = (
                (2 * degree - 1) * z * legendre[degree - 1]
                - (degree + order - 1) * legendre[degree - 2]
            ) / (degree - order)
        for degree in range(order, LMAX + 1):
            value = normalizer(degree, order) * legendre[degree]
            if order == 0:
                results[degree, 0] = value
            else:
                results[degree, order] = math.sqrt(2.0) * value * power[order].real
                results[degree, -order] = math.sqrt(2.0) * value * power[order].imag
    return results


def product_tables():
    count = 4 * COEFS
    position = np.arange(count) + 0.5
    height = 1.0 - 2.0 * position / count
    radius = np.sqrt(1.0 - height * height)
    angle = math.pi * (3.0 - math.sqrt(5.0)) * position
    points = (radius * np.cos(angle), radius * np.sin(angle), height)
    values = harmonics(*points)
    names = [(degree, m) for degree in range(LMAX + 1) for m in range(-degree, degree + 1)]
    design = np.stack([values[name] for name in names], axis=1)
    inverse = np.linalg.inv(design.T @ design) @ design.T

    def expand(samples, degree):
        fitted = inverse @ samples
        span = {m: fitted[names.index((degree, m))] for m in range(-degree, degree + 1)}
        return {m: float(v) for m, v in span.items() if abs(v) > 1e-9}

    steps = {}
    for degree in range(1, LMAX + 1):
        for m in range(-(degree - 1), degree):
            for axis in range(3):
                steps[degree, m, axis] = expand(points[axis] * values[degree - 1, m], degree)
    squares = {
        (first, second): expand(points[first] * points[second], 2)
        for first in range(3)
        for second in range(3)
    }
    linear = {axis: expand(points[axis], 1) for axis in range(3)}
    return steps, squares, linear


def row_table():
    offsets, total = {}, 0
    for order in ORDERS:
        for degree in range(abs(order), LMAX + 1):
            offsets[degree, order] = total
            total += 2 * degree + 1
    return offsets, total


OFFSETS, ENTRIES = row_table()
STEPS, SQUARES, LINEAR = product_tables()


def add_terms(terms):
    total = None
    for coefficient, value in terms:
        piece = value if coefficient == 1.0 else value * coefficient
        total = piece if total is None else total + piece
    return total


def write_rotation(vx, vy, vz, rotation):
    length = jnp.sqrt(vx * vx + vy * vy + vz * vz)
    inverse = 1.0 / length
    u = (vx * inverse, vy * inverse, vz * inverse)
    first = jnp.abs(u[0]) < 0.6
    zero = jnp.zeros_like(vx)
    a = (
        jnp.where(first, zero, -u[2]),
        jnp.where(first, u[2], zero),
        jnp.where(first, -u[1], u[0]),
    )
    scale = 1.0 / jnp.sqrt(a[0] * a[0] + a[1] * a[1] + a[2] * a[2])
    a = tuple(part * scale for part in a)
    b = (
        u[1] * a[2] - u[2] * a[1],
        u[2] * a[0] - u[0] * a[2],
        u[0] * a[1] - u[1] * a[0],
    )
    axes = {1: a, -1: b}
    for order in ORDERS:
        low = abs(order)
        if order == 0:
            row = {0: jnp.ones_like(vx)}
        elif low == 1:
            unit = -math.sqrt(2.0) * normalizer(1, 1)
            row = {}
            for m in range(-1, 2):
                row[m] = add_terms(
                    [
                        (unit * LINEAR[axis][m], axes[order][axis])
                        for axis in range(3)
                        if m in LINEAR[axis]
                    ]
                )
        else:
            unit = 3.0 * math.sqrt(2.0) * normalizer(2, 2)
            pair = {}
            for i in range(3):
                for j in range(i, 3):
                    if order == 2:
                        pair[i, j] = a[i] * a[j] - b[i] * b[j]
                        weight = 1.0 if i == j else 2.0
                    else:
                        pair[i, j] = a[i] * b[j] if i == j else a[i] * b[j] + a[j] * b[i]
                        weight = 2.0
                    pair[i, j] = (weight * unit, pair[i, j])
            row = {}
            for m in range(-2, 3):
                row[m] = add_terms(
                    [
                        (factor * SQUARES[place][m], value)
                        for place, (factor, value) in pair.items()
                        if m in SQUARES[place]
                    ]
                )
        for degree in range(low, LMAX + 1):
            if degree > low:
                gain = (
                    (2 * degree - 1)
                    / (degree - low)
                    * normalizer(degree, low)
                    / normalizer(degree - 1, low)
                )
                new = {}
                for m in range(-degree, degree + 1):
                    pieces = []
                    for axis in range(3):
                        inner = [
                            (gain * STEPS[degree, source, axis][m], row[source])
                            for source in row
                            if m in STEPS[degree, source, axis]
                        ]
                        if inner:
                            pieces.append(u[axis] * add_terms(inner))
                    new[m] = sum(pieces[1:], pieces[0])
                row = new
            for m in range(-degree, degree + 1):
                rotation[OFFSETS[degree, order] + degree + m] = row[m]
    return length


def kept(degree):
    return [order for order in ORDERS if abs(order) <= degree]


GROUPS = ((0, 1, 2, 3), (4, 5), (6,))
PAIRS = (COEFS + 1) // 2


def group_span(group):
    low = group[0] ** 2
    high = (group[-1] + 1) ** 2
    return low // 2, (high + 1) // 2


def first_row(order):
    return sum(LMAX + 1 - abs(o) for o in ORDERS[: ORDERS.index(order)])


def kernel(
    sizes,
    states,
    vectors,
    part,
    slot,
    target,
    live,
    weight_zero,
    weight_one,
    weight_two,
    out,
    w0,
    w1,
    w2,
    gathered,
    spread,
    rotation,
    sources,
    turned,
    mixer0,
    mixer1,
    mixer2,
    back,
    mixed,
    outgoing,
    incoming,
    weight_sems,
    vec_send,
    vec_recv,
    line_send,
    line_recv,
    side_send,
    side_recv,
    sum_send,
    sum_recv,
):
    parts, groups, nodes, channels, slab = sizes
    mine = lax.axis_index("edge")
    chan = lax.axis_index("chan")
    side = 2 if parts % 2 == 0 else 1
    line = parts // side
    place, flank = mine // side, mine % side
    tiles = slab // LANES
    bf16, f32 = jnp.bfloat16, jnp.float32

    weight_copies = [
        pltpu.make_async_copy(source, dest, weight_sems.at[i])
        for i, (source, dest) in enumerate(
            ((weight_zero, w0), (weight_one, w1), (weight_two, w2))
        )
    ]
    for copy in weight_copies:
        copy.start()

    for pair in range(PAIRS):
        left = states[2 * pair]
        if 2 * pair + 1 < COEFS:
            right = states[2 * pair + 1]
        else:
            right = jnp.zeros_like(left)
        gathered[mine, pair] = jnp.concatenate([left, right], axis=1)
    spread[chan] = vectors[...]

    def line_at(step):
        return ((place + step) % line) * side + flank

    across = place * side + (side - 1 - flank)
    barrier = pltpu.get_barrier_semaphore()
    met = 0
    for step in range(1, line):
        pl.semaphore_signal(barrier, 1, device_id=(line_at(step), chan), device_id_type=MESH)
        met += 1
    if side == 2:
        pl.semaphore_signal(barrier, 1, device_id=(across, chan), device_id_type=MESH)
        met += 1
    for step in range(1, groups):
        pl.semaphore_signal(
            barrier, 1, device_id=(mine, (chan + step) % groups), device_id_type=MESH
        )
        met += 1
    pl.semaphore_wait(barrier, met)

    vector_copies = []
    for step in range(1, groups):
        copy = pltpu.make_async_remote_copy(
            src_ref=vectors,
            dst_ref=spread.at[chan],
            send_sem=vec_send.at[step - 1],
            recv_sem=vec_recv.at[step - 1],
            device_id=(mine, (chan + step) % groups),
            device_id_type=MESH,
        )
        copy.start()
        vector_copies.append(copy)

    line_copies, side_copies = {}, {}
    for index, group in enumerate(GROUPS):
        low, high = group_span(group)
        span = pl.ds(low, high - low)
        for step in range(line):
            if step:
                line_copies[index, step] = pltpu.make_async_remote_copy(
                    src_ref=gathered.at[mine, span],
                    dst_ref=gathered.at[mine, span],
                    send_sem=line_send.at[index, step - 1],
                    recv_sem=line_recv.at[index, step - 1],
                    device_id=(line_at(step), chan),
                    device_id_type=MESH,
                )
            if side == 2:
                owner = line_at(line - step if step else 0)
                side_copies[index, step] = pltpu.make_async_remote_copy(
                    src_ref=gathered.at[owner, span],
                    dst_ref=gathered.at[owner, span],
                    send_sem=side_send.at[index, step],
                    recv_sem=side_recv.at[index, step],
                    device_id=(across, chan),
                    device_id_type=MESH,
                )
    for index in range(len(GROUPS)):
        for step in range(line - 1, 0, -1):
            line_copies[index, step].start()
        if side == 2:
            side_copies[index, 0].start()

    def forward(index):
        for step in range(1, line):
            line_copies[index, step].wait_recv()
            if side == 2:
                side_copies[index, step].start()

    for copy in vector_copies:
        copy.wait_recv()
    length = write_rotation(spread[:, 0, :], spread[:, 1, :], spread[:, 2, :], rotation)
    number = (
        lax.broadcasted_iota(jnp.int32, (tiles, LANES), 0) * LANES
        + lax.broadcasted_iota(jnp.int32, (tiles, LANES), 1)
    )
    envelope = 0.5 * (jnp.cos(length * (math.pi / CUTOFF)) + 1.0)
    fade = jnp.where(number < live[0], envelope, 0.0)
    forward(0)

    row = 0
    for tile in range(tiles):
        lanes = pl.ds(tile * LANES, LANES)
        hit = lax.broadcasted_iota(jnp.int32, (nodes, LANES), 0) == target[:, lanes]
        chosen = jnp.where(hit, jnp.broadcast_to(fade[tile : tile + 1], (nodes, LANES)), 0.0)
        for degree in range(LMAX + 1):
            for place_of, order in enumerate(kept(degree)):
                columns = pl.ds(place_of * slab + tile * LANES, LANES)
                for inner in range(2 * degree + 1):
                    entry = rotation[OFFSETS[degree, order] + inner, tile : tile + 1, :]
                    rows = pl.ds((degree * degree + inner) * nodes, nodes)
                    back[rows, columns] = (chosen * entry).astype(bf16)
        if tile == 0:
            forward(1)
        if tile == min(1, tiles - 1):
            forward(2)

    everyone = parts * nodes
    wanted = part[...] * nodes + slot[...]
    picker = jnp.where(
        lax.broadcasted_iota(jnp.int32, (everyone, slab), 0) == wanted, 1.0, 0.0
    ).astype(bf16)

    half = 16
    for index, group in enumerate(GROUPS):
        if side == 2:
            for step in range(line):
                side_copies[index, step].wait_recv()
        low, high = group_span(group)
        for pair in range(low, high):
            table = gathered[:, pair].reshape(everyone, 2 * channels)
            picked = lax.dot_general(
                table, picker, (((0,), (0,)), ((), ())), preferred_element_type=f32
            )
            sources[pl.ds(pair * 2 * channels, 2 * channels), :] = picked

        def turn(step, carry, group=group):
            start = pl.multiple_of((step // tiles) * half, half)
            tile = step % tiles
            lanes = pl.ds(pl.multiple_of(tile * LANES, LANES), LANES)
            for degree in group:
                totals = {}
                for inner in range(2 * degree + 1):
                    coefficient = degree * degree + inner
                    value = sources[pl.ds(coefficient * channels + start, half), lanes]
                    for order in kept(degree):
                        entry = rotation[OFFSETS[degree, order] + inner, pl.ds(tile, 1), :]
                        term = entry * value
                        totals[order] = term if inner == 0 else totals[order] + term
                for order in kept(degree):
                    at = (first_row(order) + degree - abs(order)) * channels
                    turned[pl.ds(at + start, half), lanes] = totals[order].astype(bf16)
            return carry

        lax.fori_loop(0, tiles * (channels // half), turn, 0)

    def eye(sign):
        same = lax.broadcasted_iota(jnp.int32, (slab, slab), 0) == lax.broadcasted_iota(
            jnp.int32, (slab, slab), 1
        )
        return jnp.where(same, sign, 0.0).astype(bf16)

    def flip(order):
        count = (LMAX + 1 - abs(order)) * channels
        return turned[pl.ds(first_row(order) * channels, count), :].T

    mixer0[...] = flip(0)
    for mixer, order in ((mixer1, 1), (mixer2, 2)):
        width = (LMAX + 1 - order) * channels
        plus, minus = flip(order), flip(-order)
        mixer[0:slab, 0:width] = plus
        mixer[0:slab, width : 2 * width] = -minus
        mixer[slab : 2 * slab, 0:width] = minus
        mixer[slab : 2 * slab, width : 2 * width] = plus

    for copy in weight_copies:
        copy.wait()

    width = groups * channels
    fold = LANES // channels
    sum_copies = {}
    low_lanes = lax.broadcasted_iota(jnp.int32, (1, LANES), 1) < channels
    for degree in range(LMAX, -1, -1):
        mixed[0:slab] = jnp.dot(
            mixer0[...], w0[:, degree].reshape(-1, width), preferred_element_type=f32
        ).astype(bf16)
        for order, mixer, weight in ((1, mixer1, w1), (2, mixer2, w2)):
            if degree >= order:
                at = (2 * order - 1) * slab
                mixed[at : at + 2 * slab] = jnp.dot(
                    mixer[...],
                    weight[:, :, degree - order].reshape(-1, width),
                    preferred_element_type=f32,
                ).astype(bf16)
        used = len(kept(degree)) * slab
        height = (2 * degree + 1) * nodes
        top = degree * degree * nodes
        total = jnp.dot(
            back[top : top + height, 0:used], mixed[0:used], preferred_element_type=f32
        )
        short = height // fold
        begin = top // fold
        for lump in range(width // LANES):
            block = total[:, lump * LANES : (lump + 1) * LANES]
            upper, lower = block[:short], block[short:]
            even = jnp.where(low_lanes, upper, pltpu.roll(lower, channels, 1))
            odd = jnp.where(low_lanes, pltpu.roll(upper, channels, 1), lower)
            outgoing[2 * lump, begin : begin + short] = even.astype(bf16)
            outgoing[2 * lump + 1, begin : begin + short] = odd.astype(bf16)
        for step in range(1, groups):
            peer = (chan + step) % groups
            copy = pltpu.make_async_remote_copy(
                src_ref=outgoing.at[peer, pl.ds(begin, short)],
                dst_ref=incoming.at[step - 1, pl.ds(begin, short)],
                send_sem=sum_send.at[degree, step - 1],
                recv_sem=sum_recv.at[degree, step - 1],
                device_id=(mine, peer),
                device_id_type=MESH,
            )
            copy.start()
            sum_copies[degree, step] = copy

    for degree in range(LMAX, -1, -1):
        height = (2 * degree + 1) * nodes
        top = degree * degree * nodes
        short = height // fold
        begin = top // fold
        total = outgoing[chan, begin : begin + short].astype(f32)
        for step in range(1, groups):
            sum_copies[degree, step].wait_recv()
            total = total + incoming[step - 1, begin : begin + short].astype(f32)
        out[top : top + short] = total[:, :channels].astype(bf16)
        out[top + short : top + height] = pltpu.roll(total, channels, 1)[:, :channels].astype(bf16)

    for copy in vector_copies:
        copy.wait_send()
    for copy in line_copies.values():
        copy.wait_send()
    for copy in side_copies.values():
        copy.wait_send()
    for copy in sum_copies.values():
        copy.wait_send()


def shards(
    node_states,
    edge_vectors,
    source_part,
    source_slot,
    target_slot,
    live_edges,
    weight_zero,
    weight_one,
    weight_two,
):
    slab = source_slot.shape[0]
    nodes, coefs, channels = node_states.shape
    parts = lax.axis_size("edge")
    groups = lax.axis_size("chan")
    side = 2 if parts % 2 == 0 else 1
    line = parts // side
    tiles = slab // LANES
    width = groups * channels
    bf16, f32 = jnp.bfloat16, jnp.float32
    sizes = (parts, groups, nodes, channels, slab)

    def body(*refs):
        kernel(sizes, *refs)

    vmem = pl.BlockSpec(memory_space=pltpu.VMEM)
    anywhere = pl.BlockSpec(memory_space=pl.ANY)
    zero = weight_zero.transpose(0, 2, 1, 3)
    one = weight_one.transpose(0, 1, 3, 2, 4)
    two = weight_two.transpose(0, 1, 3, 2, 4)
    dma = pltpu.SemaphoreType.DMA
    lots = len(GROUPS)
    result = pl.pallas_call(
        body,
        in_specs=[
            vmem,
            vmem,
            vmem,
            vmem,
            vmem,
            pl.BlockSpec(memory_space=pltpu.SMEM),
            anywhere,
            anywhere,
            anywhere,
        ],
        out_specs=vmem,
        out_shape=jax.ShapeDtypeStruct((coefs * nodes, channels), bf16),
        scratch_shapes=[
            pltpu.VMEM(zero.shape, bf16),
            pltpu.VMEM(one.shape, bf16),
            pltpu.VMEM(two.shape, bf16),
            pltpu.VMEM((parts, PAIRS, nodes, 2 * channels), bf16),
            pltpu.VMEM((groups, 3, slab // groups), f32),
            pltpu.VMEM((ENTRIES, tiles, LANES), f32),
            pltpu.VMEM((2 * PAIRS * channels, slab), f32),
            pltpu.VMEM(((first_row(-2) + LMAX - 1) * channels, slab), bf16),
            pltpu.VMEM((slab, (LMAX + 1) * channels), bf16),
            pltpu.VMEM((2 * slab, 2 * LMAX * channels), bf16),
            pltpu.VMEM((2 * slab, 2 * (LMAX - 1) * channels), bf16),
            pltpu.VMEM((coefs * nodes, len(ORDERS) * slab), bf16),
            pltpu.VMEM((len(ORDERS) * slab, width), bf16),
            pltpu.VMEM((groups, coefs * nodes * channels // LANES, LANES), bf16),
            pltpu.VMEM((groups - 1, coefs * nodes * channels // LANES, LANES), bf16),
            dma((3,)),
            dma((groups - 1,)),
            dma((groups - 1,)),
            dma((lots, max(line - 1, 1))),
            dma((lots, max(line - 1, 1))),
            dma((lots, line)),
            dma((lots, line)),
            dma((LMAX + 1, groups - 1)),
            dma((LMAX + 1, groups - 1)),
        ],
        compiler_params=pltpu.CompilerParams(
            collective_id=0, has_side_effects=True, vmem_limit_bytes=60 * 1024 * 1024
        ),
        name="message_layer",
    )(
        node_states.transpose(1, 0, 2),
        edge_vectors,
        source_part.reshape(1, slab),
        source_slot.reshape(1, slab),
        target_slot.reshape(1, slab),
        live_edges,
        zero,
        one,
        two,
    )
    return result.reshape(coefs, nodes, channels).transpose(1, 0, 2)


def solution(mesh):
    in_specs = (
        P("edge", None, "chan"),
        P(None, ("edge", "chan")),
        P("edge", None),
        P("edge"),
        P("edge"),
        P("edge"),
        P(None, "chan", None, None),
        P(None, None, "chan", None, None),
        P(None, None, "chan", None, None),
    )
    out_specs = P("edge", None, "chan")
    return jax.shard_map(shards, mesh=mesh, in_specs=in_specs, out_specs=out_specs, check_vma=False)
```

profile of v0, /device:TPU:0, one launch (start us, length us, event | category | flops | bytes accessed | tf_op | source)
XLA Modules:
  0.0 40.3 jit_solution(286181310761688482)
XLA Ops:
  0.7 38.1 %message_layer.1 = bf16[784,64]{1,0:T(8,128)(2,1)} custom-call(bf16[49,16,64]{2,1,0:T(8,128)(2,1)} %bitcast.14, f32[3,128]{1,0:T(4,128)} %refs_1_.1, s32[1,512]{1,0:T(1,128)} %bitcast.15, s32[1,512]{1,0:T(1,128)} %bitcast.16, s32[1,512]{1,0:T(1,128)} %bitcast.17, s32[1]{0:T(128)S(6)} %copy.11.refs_5_, bf16[7,7,64,256]{3,2,1,0:T(8,128)(2,1)} %bitcast.12, ...), custom_call_target="tpu_custom_call" | custom-call | tf_op jit(solution)/shard_map/message_layer/pallas_call | solution.py:524
  38.7 1.6 %copy.12 = bf16[16,49,64]{2,0,1:T(8,128)(2,1)} copy(bf16[16,49,64]{2,0,1:T(8,128)(2,1)} %bitcast.13) | data formatting | bytes 200704
where the time goes:
time: 40.5 us; the launch traced here: 40.3 us
  Pallas kernels  38.1 us (94%)
  local copies, waits for them, and re-layouts  1.62 us (4%)
  between operations  0.66 us (2%)
    pallas_call x1, Pallas kernels, shards(): pl.pallas_call(body, in_specs=[vmem, vmem, vmem, vmem, vmem, pl.BlockSpec...  38.1 us
    unnamed x1, local copies, waits for them, and re-layouts  1.62 us

commit v1 on v0

v1 whole, which is shorter than its diff:
```python
import math

import jax
import jax.numpy as jnp
import numpy as np
from jax import lax
from jax.experimental import pallas as pl
from jax.experimental.pallas import tpu as pltpu
from jax.sharding import PartitionSpec as P

LMAX = 6
MMAX = 2
COEFS = (LMAX + 1) ** 2
ORDERS = (0, 1, -1, 2, -2)
CUTOFF = 6.0
MESH = pl.DeviceIdType.MESH
LANES = 128


def normalizer(degree, order):
    return math.sqrt(
        (2 * degree + 1)
        / (4.0 * math.pi)
        * math.factorial(degree - order)
        / math.factorial(degree + order)
    )


def harmonics(x, y, z):
    results = {}
    power = [x * 0 + 1 + 0j]
    for _ in range(LMAX):
        power.append(power[-1] * (x + 1j * y))
    for order in range(LMAX + 1):
        start = (-1.0) ** order * math.prod(range(2 * order - 1, 0, -2))
        legendre = {order: z * 0 + start}
        if order < LMAX:
            legendre[order + 1] = (2 * order + 1) * z * start
        for degree in range(order + 2, LMAX + 1):
            legendre[degree] = (
                (2 * degree - 1) * z * legendre[degree - 1]
                - (degree + order - 1) * legendre[degree - 2]
            ) / (degree - order)
        for degree in range(order, LMAX + 1):
            value = normalizer(degree, order) * legendre[degree]
            if order == 0:
                results[degree, 0] = value
            else:
                results[degree, order] = math.sqrt(2.0) * value * power[order].real
                results[degree, -order] = math.sqrt(2.0) * value * power[order].imag
    return results


def product_tables():
    count = 4 * COEFS
    position = np.arange(count) + 0.5
    height = 1.0 - 2.0 * position / count
    radius = np.sqrt(1.0 - height * height)
    angle = math.pi * (3.0 - math.sqrt(5.0)) * position
    points = (radius * np.cos(angle), radius * np.sin(angle), height)
    values = harmonics(*points)
    names = [(degree, m) for degree in range(LMAX + 1) for m in range(-degree, degree + 1)]
    design = np.stack([values[name] for name in names], axis=1)
    inverse = np.linalg.inv(design.T @ design) @ design.T

    def expand(samples, degree):
        fitted = inverse @ samples
        span = {m: fitted[names.index((degree, m))] for m in range(-degree, degree + 1)}
        return {m: float(v) for m, v in span.items() if abs(v) > 1e-9}

    steps = {}
    for degree in range(1, LMAX + 1):
        for m in range(-(degree - 1), degree):
            for axis in range(3):
                steps[degree, m, axis] = expand(points[axis] * values[degree - 1, m], degree)
    squares = {
        (first, second): expand(points[first] * points[second], 2)
        for first in range(3)
        for second in range(3)
    }
    linear = {axis: expand(points[axis], 1) for axis in range(3)}
    return steps, squares, linear


def row_table():
    offsets, total = {}, 0
    for order in ORDERS:
        for degree in range(abs(order), LMAX + 1):
            offsets[degree, order] = total
            total += 2 * degree + 1
    return offsets, total


OFFSETS, ENTRIES = row_table()
STEPS, SQUARES, LINEAR = product_tables()


def add_terms(terms):
    total = None
    for coefficient, value in terms:
        piece = value if coefficient == 1.0 else value * coefficient
        total = piece if total is None else total + piece
    return total


def write_rotation(vx, vy, vz, rotation, orders):
    length = jnp.sqrt(vx * vx + vy * vy + vz * vz)
    inverse = 1.0 / length
    u = (vx * inverse, vy * inverse, vz * inverse)
    first = jnp.abs(u[0]) < 0.6
    zero = jnp.zeros_like(vx)
    a = (
        jnp.where(first, zero, -u[2]),
        jnp.where(first, u[2], zero),
        jnp.where(first, -u[1], u[0]),
    )
    scale = 1.0 / jnp.sqrt(a[0] * a[0] + a[1] * a[1] + a[2] * a[2])
    a = tuple(part * scale for part in a)
    b = (
        u[1] * a[2] - u[2] * a[1],
        u[2] * a[0] - u[0] * a[2],
        u[0] * a[1] - u[1] * a[0],
    )
    axes = {1: a, -1: b}
    for order in orders:
        low = abs(order)
        if order == 0:
            row = {0: jnp.ones_like(vx)}
        elif low == 1:
            unit = -math.sqrt(2.0) * normalizer(1, 1)
            row = {}
            for m in range(-1, 2):
                row[m] = add_terms(
                    [
                        (unit * LINEAR[axis][m], axes[order][axis])
                        for axis in range(3)
                        if m in LINEAR[axis]
                    ]
                )
        else:
            unit = 3.0 * math.sqrt(2.0) * normalizer(2, 2)
            pair = {}
            for i in range(3):
                for j in range(i, 3):
                    if order == 2:
                        pair[i, j] = a[i] * a[j] - b[i] * b[j]
                        weight = 1.0 if i == j else 2.0
                    else:
                        pair[i, j] = a[i] * b[j] if i == j else a[i] * b[j] + a[j] * b[i]
                        weight = 2.0
                    pair[i, j] = (weight * unit, pair[i, j])
            row = {}
            for m in range(-2, 3):
                row[m] = add_terms(
                    [
                        (factor * SQUARES[place][m], value)
                        for place, (factor, value) in pair.items()
                        if m in SQUARES[place]
                    ]
                )
        for degree in range(low, LMAX + 1):
            if degree > low:
                gain = (
                    (2 * degree - 1)
                    / (degree - low)
                    * normalizer(degree, low)
                    / normalizer(degree - 1, low)
                )
                new = {}
                for m in range(-degree, degree + 1):
                    pieces = []
                    for axis in range(3):
                        inner = [
                            (gain * STEPS[degree, source, axis][m], row[source])
                            for source in row
                            if m in STEPS[degree, source, axis]
                        ]
                        if inner:
                            pieces.append(u[axis] * add_terms(inner))
                    new[m] = sum(pieces[1:], pieces[0])
                row = new
            for m in range(-degree, degree + 1):
                rotation[OFFSETS[degree, order] + degree + m] = row[m]
    return length


def kept(degree):
    return [order for order in ORDERS if abs(order) <= degree]


GROUPS = ((0, 1, 2, 3), (4, 5), (6,))
PAIRS = (COEFS + 1) // 2
CHUNK = 32
COPIED = 16


def group_span(group):
    low = group[0] ** 2
    high = (group[-1] + 1) ** 2
    return low // 2, (high + 1) // 2


def contracted(size):
    listing, spans = [], []
    for group in GROUPS:
        begin = len(listing)
        for sign in (1, -1) if size else (1,):
            listing += [(degree, sign) for degree in group if degree >= size]
        spans.append((begin, len(listing)))
    return listing, spans


LISTS = [contracted(size) for size in range(MMAX + 1)]


def weight_plan(size):
    plan = []
    for minus in (0, 1):
        slot = 0
        for group in GROUPS:
            used = [degree for degree in group if degree >= size]
            for part in (0, 1):
                plan.append((minus, part ^ minus, used[0] - size, len(used), slot))
                slot += len(used)
    return plan


class Refs:
    pass


def kernel(sizes, names, *refs):
    r = Refs()
    for name, ref in zip(names, refs):
        setattr(r, name, ref)
    parts, groups, nodes, channels, slab = sizes
    mine = lax.axis_index("edge")
    chan = lax.axis_index("chan")
    side = 2 if parts % 2 == 0 else 1
    line = parts // side
    place, flank = mine // side, mine % side
    tiles = slab // LANES
    bf16, f32 = jnp.bfloat16, jnp.float32
    width = groups * channels
    across = place * side + (side - 1 - flank)

    def at(where):
        return where * side + flank

    loads = [
        pltpu.make_async_copy(source, dest, r.load_sems.at[k])
        for k, (source, dest) in enumerate(
            (
                (r.states_hbm, r.states),
                (r.vectors_hbm, r.vectors),
                (r.part_hbm, r.part),
                (r.slot_hbm, r.slot),
                (r.target_hbm, r.target),
                (r.live_hbm, r.live),
            )
        )
    ]
    for copy in loads:
        copy.start()

    barrier = pltpu.get_barrier_semaphore()
    reach = min(2, line - 1)
    met = 0
    for step in range(1, reach + 1):
        for way in (-1, 1):
            there = place + way * step
            present = (there >= 0) & (there < line)

            @pl.when(present)
            def _(there=there):
                pl.semaphore_signal(barrier, 1, device_id=(at(there), chan), device_id_type=MESH)

            met = met + jnp.where(present, 1, 0)
    if side == 2:
        pl.semaphore_signal(barrier, 1, device_id=(across, chan), device_id_type=MESH)
        met = met + 1
    for step in range(1, groups):
        peer = (chan + step) % groups
        pl.semaphore_signal(barrier, 1, device_id=(mine, peer), device_id_type=MESH)
        met = met + 1

    weight_copies = [pltpu.make_async_copy(r.weight_zero, r.w0, r.weight_sems.at[0])]
    for size, source, dests in (
        (1, r.weight_one, (r.plus1, r.minus1)),
        (2, r.weight_two, (r.plus2, r.minus2)),
    ):
        for minus, part, low, count, slot in weight_plan(size):
            weight_copies.append(
                pltpu.make_async_copy(
                    source.at[part, pl.ds(low, count)],
                    dests[minus].at[pl.ds(slot, count)],
                    r.weight_sems.at[len(weight_copies)],
                )
            )
    for copy in weight_copies:
        copy.start()

    loads[0].wait()
    for pair in range(PAIRS):
        left = r.states[2 * pair]
        if 2 * pair + 1 < COEFS:
            right = r.states[2 * pair + 1]
        else:
            right = jnp.zeros_like(left)
        r.gathered[mine, pair] = jnp.concatenate([left, right], axis=1)
    for copy in loads[1:]:
        copy.wait()
    r.spread[chan] = r.vectors[...]
    pl.semaphore_wait(barrier, met)

    vector_copies = []
    for step in range(1, groups):
        copy = pltpu.make_async_remote_copy(
            src_ref=r.vectors,
            dst_ref=r.spread.at[chan],
            send_sem=r.vec_send.at[step - 1],
            recv_sem=r.vec_recv.at[step - 1],
            device_id=(mine, (chan + step) % groups),
            device_id_type=MESH,
        )
        copy.start()
        vector_copies.append(copy)

    def inside(where):
        return (where >= 0) & (where < line)

    def block_of(index, owner):
        low, high = group_span(GROUPS[index])
        return r.gathered.at[owner, pl.ds(low, high - low)]

    def along(index, way, step, jump):
        kind = (0 if way > 0 else 1, step + jump - 1)
        block = block_of(index, at(place - way * step))
        return pltpu.make_async_remote_copy(
            src_ref=block,
            dst_ref=block,
            send_sem=r.line_send.at[(index, *kind)],
            recv_sem=r.line_recv.at[(index, *kind)],
            device_id=(at(place + way * jump), chan),
            device_id_type=MESH,
        )

    def over(index, way, step):
        block = block_of(index, at(place - way * step))
        number = 0 if step == 0 else 2 * step - (1 if way > 0 else 0)
        return pltpu.make_async_remote_copy(
            src_ref=block,
            dst_ref=block,
            send_sem=r.side_send.at[index, number],
            recv_sem=r.side_recv.at[index, number],
            device_id=(across, chan),
            device_id_type=MESH,
        )

    everything = []

    def launch(present, copy):
        everything.append((present, copy))

        @pl.when(present)
        def _():
            copy.start()

    for index in range(len(GROUPS)):
        for jump in range(reach, 0, -1):
            for way in (1, -1):
                launch(inside(place + way * jump), along(index, way, 0, jump))
        if side == 2:
            over(index, 1, 0).start()

    def forward(step, index):
        for way in (1, -1):
            present = inside(place - way * step)
            onward = present & inside(place + way)

            @pl.when(present)
            def _(way=way):
                along(index, way, step - 1, 1).wait_recv()
                if side == 2:
                    over(index, way, step).start()

            if step >= 2 and step < line - 1:
                launch(onward, along(index, way, step, 1))

    def arrived(index):
        if side == 2:
            over(index, 1, 0).wait_recv()
            for step in range(1, line):
                for way in (1, -1):

                    @pl.when(inside(place - way * step))
                    def _(way=way, step=step):
                        over(index, way, step).wait_recv()

    for copy in vector_copies:
        copy.wait_recv()
    number = (
        lax.broadcasted_iota(jnp.int32, (tiles, LANES), 0) * LANES
        + lax.broadcasted_iota(jnp.int32, (tiles, LANES), 1)
    )

    def prepare(step):
        if step < len(ORDERS):
            length = write_rotation(
                r.spread[:, 0, :], r.spread[:, 1, :], r.spread[:, 2, :], r.rotation, (ORDERS[step],)
            )
            if step == 0:
                envelope = 0.5 * (jnp.cos(length * (math.pi / CUTOFF)) + 1.0)
                r.fade[...] = jnp.where(number < r.live[0], envelope, 0.0)
        elif step < len(ORDERS) + tiles:
            tile = step - len(ORDERS)
            lanes = pl.ds(tile * LANES, LANES)
            hit = lax.broadcasted_iota(jnp.int32, (nodes, LANES), 0) == r.target[:, lanes]
            fading = jnp.broadcast_to(r.fade[tile : tile + 1], (nodes, LANES))
            chosen = jnp.where(hit, fading, 0.0).astype(bf16)
            for degree in range(LMAX + 1):
                for place_of, order in enumerate(kept(degree)):
                    columns = pl.ds(place_of * slab + tile * LANES, LANES)
                    for inner in range(2 * degree + 1):
                        entry = OFFSETS[degree, order] + inner
                        row = jnp.broadcast_to(
                            r.rotation[entry, tile : tile + 1, :], (COPIED, LANES)
                        ).astype(bf16)
                        r.copied[entry, :, lanes] = row
                        rows = pl.ds((degree * degree + inner) * nodes, nodes)
                        r.back[rows, columns] = chosen * row

    steps = [(step, index) for step in range(1, line) for index in range(len(GROUPS))]
    chores = len(ORDERS) + tiles
    done = 0
    for count, (step, index) in enumerate(steps):
        forward(step, index)
        while done < chores and done <= count:
            prepare(done)
            done += 1
    while done < chores:
        prepare(done)
        done += 1

    everyone = parts * nodes
    wanted = r.part[...] * nodes + r.slot[...]
    picker = jnp.where(
        lax.broadcasted_iota(jnp.int32, (everyone, slab), 0) == wanted, 1.0, 0.0
    ).astype(bf16)

    turned = (r.turned0, r.turned1, r.turned2)
    mixers = (r.mixer0, r.mixer1, r.mixer2)
    for index, group in enumerate(GROUPS):
        arrived(index)
        low, high = group_span(group)
        for pair in range(low, high):
            table = r.gathered[:, pair].reshape(everyone, 2 * channels)
            picked = lax.dot_general(
                table, picker, (((0,), (0,)), ((), ())), preferred_element_type=f32
            )
            r.sources[pl.ds(pair * 2 * channels, 2 * channels), :] = picked.astype(bf16)

        def turn(step, carry, group=group):
            start = pl.multiple_of((step // tiles) * CHUNK, CHUNK)
            lanes = pl.ds(pl.multiple_of((step % tiles) * LANES, LANES), LANES)
            for degree in group:
                totals = {}
                for inner in range(2 * degree + 1):
                    coefficient = degree * degree + inner
                    value = r.sources[pl.ds(coefficient * channels + start, CHUNK), lanes]
                    value = value.reshape(CHUNK // COPIED, COPIED, LANES)
                    for order in kept(degree):
                        entry = r.copied[OFFSETS[degree, order] + inner, :, lanes]
                        term = entry[None] * value
                        totals[order] = term if inner == 0 else totals[order] + term
                for order in kept(degree):
                    sign = -1 if order < 0 else 1
                    row = LISTS[abs(order)][0].index((degree, sign)) * channels
                    turned[abs(order)][pl.ds(row + start, CHUNK), lanes] = totals[order].reshape(
                        CHUNK, LANES
                    )
            return carry

        lax.fori_loop(0, tiles * (channels // CHUNK), turn, 0)
        for size in range(MMAX + 1):
            begin, end = (n * channels for n in LISTS[size][1][index])
            mixers[size][:, begin:end] = turned[size][begin:end, :].T

    for copy in weight_copies:
        copy.wait()
    for size, weights in ((1, r.plus1), (2, r.plus2)):
        for slot, (_, sign) in enumerate(LISTS[size][0]):
            if sign < 0:
                weights[slot] = -weights[slot]

    fold = LANES // channels
    low_lanes = lax.broadcasted_iota(jnp.int32, (1, LANES), 1) < channels

    def span_of(degree):
        height = (2 * degree + 1) * nodes
        top = degree * degree * nodes
        return top, height, top // fold, height // fold

    def convolve(degree):
        keep = degree % 2
        for number, order in enumerate(kept(degree)):
            size = abs(order)
            if size == 0:
                weight = r.w0[:, degree]
            else:
                source = ((r.minus1, r.plus1), (r.minus2, r.plus2))[size - 1][order > 0]
                weight = source[:, degree - size]
            r.mixed[keep, number * slab : (number + 1) * slab] = jnp.dot(
                mixers[size][...], weight.reshape(-1, width), preferred_element_type=f32
            ).astype(bf16)

    def gather_back(degree):
        used = len(kept(degree)) * slab
        top, height, begin, short = span_of(degree)
        total = jnp.dot(
            r.back[top : top + height, 0:used],
            r.mixed[degree % 2, 0:used],
            preferred_element_type=f32,
        )
        for lump in range(width // LANES):
            block = total[:, lump * LANES : (lump + 1) * LANES]
            upper, lower = block[:short], block[short:]
            even = jnp.where(low_lanes, upper, pltpu.roll(lower, channels, 1))
            odd = jnp.where(low_lanes, pltpu.roll(upper, channels, 1), lower)
            r.outgoing[2 * lump, begin : begin + short] = even.astype(bf16)
            r.outgoing[2 * lump + 1, begin : begin + short] = odd.astype(bf16)

    sum_copies = {}

    def send(degree):
        _, _, begin, short = span_of(degree)
        for step in range(1, groups):
            peer = (chan + step) % groups
            copy = pltpu.make_async_remote_copy(
                src_ref=r.outgoing.at[peer, pl.ds(begin, short)],
                dst_ref=r.incoming.at[step - 1, pl.ds(begin, short)],
                send_sem=r.sum_send.at[degree, step - 1],
                recv_sem=r.sum_recv.at[degree, step - 1],
                device_id=(mine, peer),
                device_id_type=MESH,
            )
            copy.start()
            sum_copies[degree, step] = copy

    for degree in range(LMAX, -1, -1):
        if degree + 2 <= LMAX:
            send(degree + 2)
        convolve(degree)
        if degree + 1 <= LMAX:
            gather_back(degree + 1)
    send(1)
    gather_back(0)
    send(0)

    for degree in range(LMAX, -1, -1):
        top, height, begin, short = span_of(degree)
        total = r.outgoing[chan, begin : begin + short].astype(f32)
        for step in range(1, groups):
            sum_copies[degree, step].wait_recv()
            total = total + r.incoming[step - 1, begin : begin + short].astype(f32)
        r.out[top : top + short] = total[:, :channels].astype(bf16)
        r.out[top + short : top + height] = pltpu.roll(total, channels, 1)[:, :channels].astype(
            bf16
        )

    for copy in vector_copies:
        copy.wait_send()
    for present, copy in everything:

        @pl.when(present)
        def _(copy=copy):
            copy.wait_send()

    if side == 2:
        for index in range(len(GROUPS)):
            over(index, 1, 0).wait_send()
            for step in range(1, line):
                for way in (1, -1):

                    @pl.when(inside(place - way * step))
                    def _(index=index, way=way, step=step):
                        over(index, way, step).wait_send()

    for copy in sum_copies.values():
        copy.wait_send()


def shards(
    node_states,
    edge_vectors,
    source_part,
    source_slot,
    target_slot,
    live_edges,
    weight_zero,
    weight_one,
    weight_two,
):
    slab = source_slot.shape[0]
    nodes, coefs, channels = node_states.shape
    parts = lax.axis_size("edge")
    groups = lax.axis_size("chan")
    line = parts // (2 if parts % 2 == 0 else 1)
    tiles = slab // LANES
    width = groups * channels
    bf16, f32, i32 = jnp.bfloat16, jnp.float32, jnp.int32
    zero = weight_zero.transpose(0, 2, 1, 3)
    one = weight_one.transpose(0, 1, 3, 2, 4)
    two = weight_two.transpose(0, 1, 3, 2, 4)
    operands = dict(
        states_hbm=node_states.transpose(1, 0, 2),
        vectors_hbm=edge_vectors,
        part_hbm=source_part.reshape(1, slab),
        slot_hbm=source_slot.reshape(1, slab),
        target_hbm=target_slot.reshape(1, slab),
        live_hbm=live_edges,
        weight_zero=zero,
        weight_one=one,
        weight_two=two,
    )
    dma = pltpu.SemaphoreType.DMA
    vmem = pltpu.VMEM
    lots = len(GROUPS)
    rows = [len(listing) * channels for listing, _ in LISTS]
    hops = max(line - 1, 1)
    folded = coefs * nodes * channels // LANES
    weight_shape = [(len(listing),) for listing, _ in LISTS]
    scratch = dict(
        states=vmem((coefs, nodes, channels), bf16),
        vectors=vmem(edge_vectors.shape, f32),
        part=vmem((1, slab), i32),
        slot=vmem((1, slab), i32),
        target=vmem((1, slab), i32),
        live=pltpu.SMEM((1,), i32),
        w0=vmem(zero.shape, bf16),
        plus1=vmem(weight_shape[1] + one.shape[2:], bf16),
        minus1=vmem(weight_shape[1] + one.shape[2:], bf16),
        plus2=vmem(weight_shape[2] + two.shape[2:], bf16),
        minus2=vmem(weight_shape[2] + two.shape[2:], bf16),
        gathered=vmem((parts, PAIRS, nodes, 2 * channels), bf16),
        spread=vmem((groups, 3, slab // groups), f32),
        rotation=vmem((ENTRIES, tiles, LANES), f32),
        fade=vmem((tiles, LANES), f32),
        copied=vmem((ENTRIES, COPIED, slab), bf16),
        sources=vmem((2 * PAIRS * channels, slab), bf16),
        turned0=vmem((rows[0], slab), bf16),
        turned1=vmem((rows[1], slab), bf16),
        turned2=vmem((rows[2], slab), bf16),
        mixer0=vmem((slab, rows[0]), bf16),
        mixer1=vmem((slab, rows[1]), bf16),
        mixer2=vmem((slab, rows[2]), bf16),
        back=vmem((coefs * nodes, len(ORDERS) * slab), bf16),
        mixed=vmem((2, len(ORDERS) * slab, width), bf16),
        outgoing=vmem((groups, folded, LANES), bf16),
        incoming=vmem((groups - 1, folded, LANES), bf16),
        load_sems=dma((6,)),
        weight_sems=dma((1 + len(weight_plan(1)) + len(weight_plan(2)),)),
        vec_send=dma((groups - 1,)),
        vec_recv=dma((groups - 1,)),
        line_send=dma((lots, 2, hops)),
        line_recv=dma((lots, 2, hops)),
        side_send=dma((lots, 2 * line - 1)),
        side_recv=dma((lots, 2 * line - 1)),
        sum_send=dma((LMAX + 1, groups - 1)),
        sum_recv=dma((LMAX + 1, groups - 1)),
    )
    names = [*operands, "out", *scratch]
    sizes = (parts, groups, nodes, channels, slab)

    def body(*refs):
        kernel(sizes, names, *refs)

    result = pl.pallas_call(
        body,
        in_specs=[pl.BlockSpec(memory_space=pl.ANY)] * len(operands),
        out_specs=pl.BlockSpec(memory_space=pltpu.VMEM),
        out_shape=jax.ShapeDtypeStruct((coefs * nodes, channels), bf16),
        scratch_shapes=list(scratch.values()),
        compiler_params=pltpu.CompilerParams(
            collective_id=0, has_side_effects=True, vmem_limit_bytes=48 * 1024 * 1024
        ),
        name="message_layer",
    )(*operands.values())
    return result.reshape(coefs, nodes, channels).transpose(1, 0, 2)


def solution(mesh):
    in_specs = (
        P("edge", None, "chan"),
        P(None, ("edge", "chan")),
        P("edge", None),
        P("edge"),
        P("edge"),
        P("edge"),
        P(None, "chan", None, None),
        P(None, None, "chan", None, None),
        P(None, None, "chan", None, None),
    )
    out_specs = P("edge", None, "chan")
    return jax.shard_map(shards, mesh=mesh, in_specs=in_specs, out_specs=out_specs, check_vma=False)
```

time: 40.5 us -> 51.5 us (1.27)
  local copies, waits for them, and re-layouts: 1.62 us -> 8.84 us
  Pallas kernels: 38.1 us -> 41.6 us
    unnamed x1 -> x17, local copies, waits for them, and re-layouts: 1.62 us -> 8.84 us
    pallas_call x1, Pallas kernels: 38.1 us -> 41.6 us  [shards(): pl.pallas_call(body, in_specs=[pl.BlockSpec(memory_space=pl.ANY)] * len(o...]
where the time goes in v1:
time: 51.5 us; the launch traced here: 51.2 us
  Pallas kernels  41.6 us (81%)
  local copies, waits for them, and re-layouts  8.84 us (17%)
  between operations  0.68 us (1%)
    pallas_call x1, Pallas kernels, shards(): pl.pallas_call(body, in_specs=[pl.BlockSpec(memory_space=pl.ANY)] * len(o...  41.6 us
    unnamed x17, local copies, waits for them, and re-layouts  8.84 us

profile of v1, /device:TPU:0, one launch (start us, length us, event | category | flops | bytes accessed | tf_op | source)
XLA Modules:
  0.0 51.2 jit_solution(2212147752149278763)
XLA Ops:
  0.7 0.0 copy-start
  0.7 1.7 %copy-done = bf16[2,6,64,6,256]{4,2,3,1,0:T(8,128)(2,1)S(1)} copy-done((bf16[2,6,64,6,256]{4,2,3,1,0:T(8,128)(2,1)S(1)}, bf16[2,6,64,6,256]{4,2,3,1,0:T(8,128)(2,1)}, u32[]{:S(2)}) %copy-start) | copy-done | bytes 2359320
  2.3 0.0 copy-start.1
  2.3 1.4 %copy-done.1 = bf16[2,5,64,5,256]{4,2,3,1,0:T(8,128)(2,1)S(1)} copy-done((bf16[2,5,64,5,256]{4,2,3,1,0:T(8,128)(2,1)S(1)}, bf16[2,5,64,5,256]{4,2,3,1,0:T(8,128)(2,1)}, u32[]{:S(2)}) %copy-start.1) | copy-done | bytes 1638424
  3.7 0.0 copy-start.2
  3.8 1.4 %copy-done.2 = bf16[7,64,7,256]{3,1,2,0:T(8,128)(2,1)S(1)} copy-done((bf16[7,64,7,256]{3,1,2,0:T(8,128)(2,1)S(1)}, bf16[7,64,7,256]{3,1,2,0:T(8,128)(2,1)}, u32[]{:S(2)}) %copy-start.2) | copy-done | bytes 1605656
  5.2 0.0 copy-start.3
  5.2 0.9 %copy-done.3 = bf16[16,49,64]{2,0,1:T(8,128)(2,1)S(1)} copy-done((bf16[16,49,64]{2,0,1:T(8,128)(2,1)S(1)}, bf16[16,49,64]{2,0,1:T(8,128)(2,1)}, u32[]{:S(2)}) %copy-start.3) | copy-done | bytes 100376
  6.1 0.0 copy-start.4
  6.1 0.7 %copy-done.4 = f32[3,128]{1,0:T(4,128)S(1)} copy-done((f32[3,128]{1,0:T(4,128)S(1)}, f32[3,128]{1,0:T(4,128)}, u32[]{:S(2)}) %copy-start.4) | copy-done | bytes 1560
  6.8 0.0 copy-start.5
  6.8 0.7 %copy-done.5 = s32[512,1]{0,1:T(1,128)S(1)} copy-done((s32[512,1]{0,1:T(1,128)S(1)}, s32[512,1]{0,1:T(1,128)}, u32[]{:S(2)}) %copy-start.5) | copy-done | bytes 2072
  7.5 0.0 copy-start.6
  7.5 0.7 %copy-done.6 = s32[512]{0:T(512)S(1)} copy-done((s32[512]{0:T(512)S(1)}, s32[512]{0:T(512)}, u32[]{:S(2)}) %copy-start.6) | copy-done | bytes 2072
  8.1 0.0 copy-start.7
  8.1 0.7 %copy-done.7 = s32[512]{0:T(512)S(1)} copy-done((s32[512]{0:T(512)S(1)}, s32[512]{0:T(512)}, u32[]{:S(2)}) %copy-start.7) | copy-done | bytes 2072
  8.8 41.6 %message_layer.1 = bf16[784,64]{1,0:T(8,128)(2,1)S(1)} custom-call(bf16[49,16,64]{2,1,0:T(8,128)(2,1)S(1)} %bitcast.14, f32[3,128]{1,0:T(4,128)S(1)} %copy-done.4, s32[1,512]{1,0:T(1,128)S(1)} %bitcast.15, s32[1,512]{1,0:T(1,128)S(1)} %bitcast.16, s32[1,512]{1,0:T(1,128)S(1)} %bitcast.17, s32[1]{0:T(128)S(6)} %copy.11.refs_5_, ...), custom_call_target="tpu_custom_call" | custom-call | tf_op jit(solution)/shard_map/message_layer/pallas_call | solution.py:678
  50.5 0.7 %copy.12 = bf16[16,49,64]{2,0,1:T(8,128)(2,1)} copy(bf16[16,49,64]{2,0,1:T(8,128)(2,1)S(1)} %bitcast.13) | data formatting | bytes 200704
Async XLA Ops:
  0.7 1.7 %copy-start = (bf16[2,6,64,6,256]{4,2,3,1,0:T(8,128)(2,1)S(1)}, bf16[2,6,64,6,256]{4,2,3,1,0:T(8,128)(2,1)}, u32[]{:S(2)}) copy-start(bf16[2,6,64,6,256]{4,2,3,1,0:T(8,128)(2,1)} %param.16) | copy-start | bytes 7077892
  2.3 1.4 %copy-start.1 = (bf16[2,5,64,5,256]{4,2,3,1,0:T(8,128)(2,1)S(1)}, bf16[2,5,64,5,256]{4,2,3,1,0:T(8,128)(2,1)}, u32[]{:S(2)}) copy-start(bf16[2,5,64,5,256]{4,2,3,1,0:T(8,128)(2,1)} %param.17) | copy-start | bytes 4915204
  3.7 1.4 %copy-start.2 = (bf16[7,64,7,256]{3,1,2,0:T(8,128)(2,1)S(1)}, bf16[7,64,7,256]{3,1,2,0:T(8,128)(2,1)}, u32[]{:S(2)}) copy-start(bf16[7,64,7,256]{3,1,2,0:T(8,128)(2,1)} %param.15) | copy-start | bytes 4816900
  5.2 0.9 %copy-start.3 = (bf16[16,49,64]{2,0,1:T(8,128)(2,1)S(1)}, bf16[16,49,64]{2,0,1:T(8,128)(2,1)}, u32[]{:S(2)}) copy-start(bf16[16,49,64]{2,0,1:T(8,128)(2,1)} %param.9) | copy-start | bytes 301060
  6.1 0.7 %copy-start.4 = (f32[3,128]{1,0:T(4,128)S(1)}, f32[3,128]{1,0:T(4,128)}, u32[]{:S(2)}) copy-start(f32[3,128]{1,0:T(4,128)} %refs_1_.1) | copy-start | bytes 4612
  6.8 0.7 %copy-start.5 = (s32[512,1]{0,1:T(1,128)S(1)}, s32[512,1]{0,1:T(1,128)}, u32[]{:S(2)}) copy-start(s32[512,1]{0,1:T(1,128)} %param.11) | copy-start | bytes 6148
  7.5 0.7 %copy-start.6 = (s32[512]{0:T(512)S(1)}, s32[512]{0:T(512)}, u32[]{:S(2)}) copy-start(s32[512]{0:T(512)} %param.12) | copy-start | bytes 6148
  8.1 0.7 %copy-start.7 = (s32[512]{0:T(512)S(1)}, s32[512]{0:T(512)}, u32[]{:S(2)}) copy-start(s32[512]{0:T(512)} %param.13) | copy-start | bytes 6148
